TPU v7x, 32 devices: a whole 2x2x4 slice. The times are simulated.
32 devices in a mesh: gx: 4 (over x, core), gy: 4 (over z), gz: 2 (over y).
Axes of the slice: x: 2, y: 2, z: 4, core: 2. Of those that a mesh axis runs over, the one named last changes fastest.
Arguments:
- columns: int32 [1024, 2048], P(('gx', 'gy', 'gz')), may hold values from 0 to 32767, as said below
- counts: int32 [1024, 2048], P(('gx', 'gy', 'gz')), may hold values from 1 to 63
- nnz_count: int32 [1024], P(('gx', 'gy', 'gz')), may hold values from 1 to 2048, as said below
- selected: int32 [2048], replicated, may hold values from 0 to 32767, as said below
Outputs:
- gene_stats: float32 [2, 32768], P(None, 'gz')
- pca_input: bfloat16 [1024, 2048], P(('gx', 'gy'), 'gz')
Inputs may be any that keep to these rules, and one draw needn't show every extreme that they name: `columns`: in each row no two slots fall in the same block of 16 consecutive genes (so the first nnz_count slots hold distinct genes); slots beyond nnz_count are not part of the matrix. For every k, the live slots of one cell fall on at most 128 of the genes selected[k * 2048 / 2] to selected[(k + 1) * 2048 / 2 - 1]; some cell reaches 128 for every k in every draw. `nnz_count`: some cell has all 2048 slots live in every draw. `selected`: distinct genes.
All inputs are finite; a program needn't handle non-finite values.
Results may differ from a plain program's by a relative error of at most 0.0085.
Values may be sent and summed in bfloat16 or wider, within the bound.
No kernel may reach another device: no remote copies, remote signals or barrier semaphores. Data moves between devices by JAX's collectives and lax.ppermute only.
A program may use at most 128 MiB of HBM per device.

v0:
```python
import jax
import jax.numpy as jnp
from jax import lax
from jax.sharding import PartitionSpec as P

GENES = 32768
SEL = 2048
target_sum = 10000.0
var_floor = 0.01
clip_value = 10.0
lane_count = 256


def standardize(dense, mean_sel, variance_sel):
    scale_sel = jnp.sqrt(jnp.maximum(variance_sel, var_floor))
    return jnp.clip((dense - mean_sel[None, :]) / scale_sel[None, :], -clip_value, clip_value)


def cell_block(pair):
    block_genes, block_values = pair
    high_count = GENES // lane_count
    high_ids = lax.broadcasted_iota(jnp.int32, (1, 1, high_count), 2)
    low_ids = lax.broadcasted_iota(jnp.int32, (1, 1, lane_count), 2)
    high_table = ((block_genes // lane_count)[:, :, None] == high_ids).astype(jnp.bfloat16)
    low_hit = (block_genes % lane_count)[:, :, None] == low_ids
    upper = lax.optimization_barrier(block_values.astype(jnp.bfloat16))
    lower = (block_values - upper.astype(jnp.float32)).astype(jnp.bfloat16)
    upper_table = jnp.where(low_hit, upper[:, :, None], jnp.bfloat16(0.0))
    lower_table = jnp.where(low_hit, lower[:, :, None], jnp.bfloat16(0.0))
    upper_part = jnp.einsum(
        "csh,csl->chl", high_table, upper_table, preferred_element_type=jnp.float32
    )
    lower_part = jnp.einsum(
        "csh,csl->chl", high_table, lower_table, preferred_element_type=jnp.float32
    )
    return upper_part + lower_part


def per_device(columns, counts, nnz_count, selected):
    local_cells = columns.shape[0]
    row_slots = columns.shape[1]
    owners = lax.axis_size("gz")
    owner_index = lax.axis_index("gz")
    cells = local_cells * lax.axis_size("gx") * lax.axis_size("gy") * owners
    slot = lax.broadcasted_iota(jnp.int32, counts.shape, 1)
    live = slot < nnz_count[:, None]
    raw = jnp.where(live, counts.astype(jnp.float32), jnp.float32(0.0))
    library = jnp.sum(raw, axis=1, keepdims=True)
    values = jnp.log1p(raw * (target_sum / library))
    genes = jnp.where(live, columns, 0)
    block_rows = 4
    block_total = local_cells // block_rows
    expanded = lax.map(
        cell_block,
        (
            genes.reshape(block_total, block_rows, row_slots),
            values.reshape(block_total, block_rows, row_slots),
        ),
    )
    expanded = expanded.reshape(local_cells, GENES)
    total = jnp.sum(expanded, axis=0)
    square = jnp.sum(expanded * expanded, axis=0)
    terms = jnp.stack([total, square])
    owned = GENES // owners
    sums = lax.psum(terms, ("gx", "gy", "gz"))
    own_sums = lax.dynamic_slice_in_dim(sums, owner_index * owned, owned, 1)
    picked_sums = jnp.take(sums, selected, axis=1)
    own_mean = own_sums[0] / cells
    own_variance = own_sums[1] / cells - own_mean * own_mean
    gene_stats = jnp.stack([own_mean, own_variance])
    sel_mean = picked_sums[0] / cells
    sel_variance = picked_sums[1] / cells - sel_mean * sel_mean
    dense = jnp.take(expanded, selected, axis=1)
    share_size = SEL // owners
    own_mean_sel = lax.dynamic_slice_in_dim(sel_mean, owner_index * share_size, share_size, 0)
    own_variance_sel = lax.dynamic_slice_in_dim(
        sel_variance, owner_index * share_size, share_size, 0
    )
    moved = lax.all_to_all(
        dense.astype(jnp.bfloat16), "gz", split_axis=1, concat_axis=0, tiled=True
    ).astype(dense.dtype)
    pca_input = standardize(moved, own_mean_sel, own_variance_sel).astype(jnp.bfloat16)
    return (gene_stats, pca_input)


def solution(mesh):
    return jax.shard_map(
        per_device,
        mesh=mesh,
        in_specs=(
            P(("gx", "gy", "gz"), None),
            P(("gx", "gy", "gz"), None),
            P(("gx", "gy", "gz")),
            P(),
        ),
        out_specs=(P(None, "gz"), P(("gx", "gy"), "gz")),
        check_vma=False,
    )
```

profile of v0, /device:TPU:0, one launch (start us, length us, event | category | flops | bytes accessed | tf_op | source)
XLA Modules:
  0.0 230.8 jit_solution(16225255947262282294)
XLA Ops:
  7.2 1.2 fusion.36
  8.4 1.1 multiply_log-plus-one_fusion
  9.6 1.0 fusion.35
  10.8 56.9 %while.12 = (s32[]{:T(128)}, f32[8,4,128,256]{3,2,1,0:T(8,128)}, s32[8,4,2048]{2,1,0:T(4,128)S(1)}, f32[8,4,2048]{2,1,0:T(4,128)S(1)}, s32[]{:T(128)}) while((s32[]{:T(128)}, f32[8,4,128,256]{3,2,1,0:T(8,128)}, s32[8,4,2048]{2,1,0:T(4,128)S(1)}, f32[8,4,2048]{2,1,0:T(4,128)S(1)}, s32[]{:T(128)}) %tuple.39), condition=%wide.region_2.3_spmd, body=%wide.region_1.2_spmd.sunk | while | flops 1084588032 | bytes 1982553 | solution.py:53
  10.9 3.2 %fusion.48 = f32[4,128,256]{2,1,0:T(8,128)S(1)} fusion(s32[4,2048]{1,0:T(4,128)S(1)} %add_select_fusion.5, bf16[4,2048]{1,0:T(4,128)(2,1)S(1)} %bitcast_convert_fusion.2, s32[4,2048]{1,0:T(4,128)S(1)} %get-tuple-element.109), kind=kOutput, calls=%fused_computation.5.clone.1 | convolution fusion | flops 542113792 | bytes 606208 | tf_op jit(solution)/shard_map/while/body/eval_jaxpr/csh,csl->chl/dot_general | solution.py:30
  14.1 3.8 %fusion.50 = f32[8,4,128,256]{3,2,1,0:T(8,128)} fusion(f32[8,4,128,256]{3,2,1,0:T(8,128)} %get-tuple-element.116, s32[]{:T(128)S(6)} %copy.30, f32[4,128,256]{2,1,0:T(8,128)S(1)} %fusion.48, s32[4,2048]{1,0:T(4,128)S(1)} %add_select_fusion.5, bf16[4,2048]{1,0:T(4,128)(2,1)S(1)} %fusion.49, s32[4,2048]{1,0:T(4,128)S(1)} %get-tuple-element.109), kind=kOutput, calls=%fused_computation.18.clone.1 | convolution fusion | flops 542244864 | bytes 1130500 | tf_op jit(solution)/shard_map/while/body/eval_jaxpr/csh,csl->chl/dot_general | solution.py:33
  18.0 3.2 %fusion.48 = f32[4,128,256]{2,1,0:T(8,128)S(1)} fusion(s32[4,2048]{1,0:T(4,128)S(1)} %add_select_fusion.5, bf16[4,2048]{1,0:T(4,128)(2,1)S(1)} %bitcast_convert_fusion.2, s32[4,2048]{1,0:T(4,128)S(1)} %get-tuple-element.109), kind=kOutput, calls=%fused_computation.5.clone.1 | convolution fusion | flops 542113792 | bytes 606208 | tf_op jit(solution)/shard_map/while/body/eval_jaxpr/csh,csl->chl/dot_general | solution.py:30
  21.2 3.8 %fusion.50 = f32[8,4,128,256]{3,2,1,0:T(8,128)} fusion(f32[8,4,128,256]{3,2,1,0:T(8,128)} %get-tuple-element.116, s32[]{:T(128)S(6)} %copy.30, f32[4,128,256]{2,1,0:T(8,128)S(1)} %fusion.48, s32[4,2048]{1,0:T(4,128)S(1)} %add_select_fusion.5, bf16[4,2048]{1,0:T(4,128)(2,1)S(1)} %fusion.49, s32[4,2048]{1,0:T(4,128)S(1)} %get-tuple-element.109), kind=kOutput, calls=%fused_computation.18.clone.1 | convolution fusion | flops 542244864 | bytes 1130500 | tf_op jit(solution)/shard_map/while/body/eval_jaxpr/csh,csl->chl/dot_general | solution.py:33
  25.1 3.2 %fusion.48 = f32[4,128,256]{2,1,0:T(8,128)S(1)} fusion(s32[4,2048]{1,0:T(4,128)S(1)} %add_select_fusion.5, bf16[4,2048]{1,0:T(4,128)(2,1)S(1)} %bitcast_convert_fusion.2, s32[4,2048]{1,0:T(4,128)S(1)} %get-tuple-element.109), kind=kOutput, calls=%fused_computation.5.clone.1 | convolution fusion | flops 542113792 | bytes 606208 | tf_op jit(solution)/shard_map/while/body/eval_jaxpr/csh,csl->chl/dot_general | solution.py:30
  28.3 3.8 %fusion.50 = f32[8,4,128,256]{3,2,1,0:T(8,128)} fusion(f32[8,4,128,256]{3,2,1,0:T(8,128)} %get-tuple-element.116, s32[]{:T(128)S(6)} %copy.30, f32[4,128,256]{2,1,0:T(8,128)S(1)} %fusion.48, s32[4,2048]{1,0:T(4,128)S(1)} %add_select_fusion.5, bf16[4,2048]{1,0:T(4,128)(2,1)S(1)} %fusion.49, s32[4,2048]{1,0:T(4,128)S(1)} %get-tuple-element.109), kind=kOutput, calls=%fused_computation.18.clone.1 | convolution fusion | flops 542244864 | bytes 1130500 | tf_op jit(solution)/shard_map/while/body/eval_jaxpr/csh,csl->chl/dot_general | solution.py:33
  32.3 3.2 %fusion.48 = f32[4,128,256]{2,1,0:T(8,128)S(1)} fusion(s32[4,2048]{1,0:T(4,128)S(1)} %add_select_fusion.5, bf16[4,2048]{1,0:T(4,128)(2,1)S(1)} %bitcast_convert_fusion.2, s32[4,2048]{1,0:T(4,128)S(1)} %get-tuple-element.109), kind=kOutput, calls=%fused_computation.5.clone.1 | convolution fusion | flops 542113792 | bytes 606208 | tf_op jit(solution)/shard_map/while/body/eval_jaxpr/csh,csl->chl/dot_general | solution.py:30
  35.4 3.8 %fusion.50 = f32[8,4,128,256]{3,2,1,0:T(8,128)} fusion(f32[8,4,128,256]{3,2,1,0:T(8,128)} %get-tuple-element.116, s32[]{:T(128)S(6)} %copy.30, f32[4,128,256]{2,1,0:T(8,128)S(1)} %fusion.48, s32[4,2048]{1,0:T(4,128)S(1)} %add_select_fusion.5, bf16[4,2048]{1,0:T(4,128)(2,1)S(1)} %fusion.49, s32[4,2048]{1,0:T(4,128)S(1)} %get-tuple-element.109), kind=kOutput, calls=%fused_computation.18.clone.1 | convolution fusion | flops 542244864 | bytes 1130500 | tf_op jit(solution)/shard_map/while/body/eval_jaxpr/csh,csl->chl/dot_general | solution.py:33
  39.4 3.2 %fusion.48 = f32[4,128,256]{2,1,0:T(8,128)S(1)} fusion(s32[4,2048]{1,0:T(4,128)S(1)} %add_select_fusion.5, bf16[4,2048]{1,0:T(4,128)(2,1)S(1)} %bitcast_convert_fusion.2, s32[4,2048]{1,0:T(4,128)S(1)} %get-tuple-element.109), kind=kOutput, calls=%fused_computation.5.clone.1 | convolution fusion | flops 542113792 | bytes 606208 | tf_op jit(solution)/shard_map/while/body/eval_jaxpr/csh,csl->chl/dot_general | solution.py:30
  42.5 3.8 %fusion.50 = f32[8,4,128,256]{3,2,1,0:T(8,128)} fusion(f32[8,4,128,256]{3,2,1,0:T(8,128)} %get-tuple-element.116, s32[]{:T(128)S(6)} %copy.30, f32[4,128,256]{2,1,0:T(8,128)S(1)} %fusion.48, s32[4,2048]{1,0:T(4,128)S(1)} %add_select_fusion.5, bf16[4,2048]{1,0:T(4,128)(2,1)S(1)} %fusion.49, s32[4,2048]{1,0:T(4,128)S(1)} %get-tuple-element.109), kind=kOutput, calls=%fused_computation.18.clone.1 | convolution fusion | flops 542244864 | bytes 1130500 | tf_op jit(solution)/shard_map/while/body/eval_jaxpr/csh,csl->chl/dot_general | solution.py:33
  46.5 3.2 %fusion.48 = f32[4,128,256]{2,1,0:T(8,128)S(1)} fusion(s32[4,2048]{1,0:T(4,128)S(1)} %add_select_fusion.5, bf16[4,2048]{1,0:T(4,128)(2,1)S(1)} %bitcast_convert_fusion.2, s32[4,2048]{1,0:T(4,128)S(1)} %get-tuple-element.109), kind=kOutput, calls=%fused_computation.5.clone.1 | convolution fusion | flops 542113792 | bytes 606208 | tf_op jit(solution)/shard_map/while/body/eval_jaxpr/csh,csl->chl/dot_general | solution.py:30
  49.6 3.8 %fusion.50 = f32[8,4,128,256]{3,2,1,0:T(8,128)} fusion(f32[8,4,128,256]{3,2,1,0:T(8,128)} %get-tuple-element.116, s32[]{:T(128)S(6)} %copy.30, f32[4,128,256]{2,1,0:T(8,128)S(1)} %fusion.48, s32[4,2048]{1,0:T(4,128)S(1)} %add_select_fusion.5, bf16[4,2048]{1,0:T(4,128)(2,1)S(1)} %fusion.49, s32[4,2048]{1,0:T(4,128)S(1)} %get-tuple-element.109), kind=kOutput, calls=%fused_computation.18.clone.1 | convolution fusion | flops 542244864 | bytes 1130500 | tf_op jit(solution)/shard_map/while/body/eval_jaxpr/csh,csl->chl/dot_general | solution.py:33
  53.6 3.2 %fusion.48 = f32[4,128,256]{2,1,0:T(8,128)S(1)} fusion(s32[4,2048]{1,0:T(4,128)S(1)} %add_select_fusion.5, bf16[4,2048]{1,0:T(4,128)(2,1)S(1)} %bitcast_convert_fusion.2, s32[4,2048]{1,0:T(4,128)S(1)} %get-tuple-element.109), kind=kOutput, calls=%fused_computation.5.clone.1 | convolution fusion | flops 542113792 | bytes 606208 | tf_op jit(solution)/shard_map/while/body/eval_jaxpr/csh,csl->chl/dot_general | solution.py:30
  56.7 3.8 %fusion.50 = f32[8,4,128,256]{3,2,1,0:T(8,128)} fusion(f32[8,4,128,256]{3,2,1,0:T(8,128)} %get-tuple-element.116, s32[]{:T(128)S(6)} %copy.30, f32[4,128,256]{2,1,0:T(8,128)S(1)} %fusion.48, s32[4,2048]{1,0:T(4,128)S(1)} %add_select_fusion.5, bf16[4,2048]{1,0:T(4,128)(2,1)S(1)} %fusion.49, s32[4,2048]{1,0:T(4,128)S(1)} %get-tuple-element.109), kind=kOutput, calls=%fused_computation.18.clone.1 | convolution fusion | flops 542244864 | bytes 1130500 | tf_op jit(solution)/shard_map/while/body/eval_jaxpr/csh,csl->chl/dot_general | solution.py:33
  60.7 3.2 %fusion.48 = f32[4,128,256]{2,1,0:T(8,128)S(1)} fusion(s32[4,2048]{1,0:T(4,128)S(1)} %add_select_fusion.5, bf16[4,2048]{1,0:T(4,128)(2,1)S(1)} %bitcast_convert_fusion.2, s32[4,2048]{1,0:T(4,128)S(1)} %get-tuple-element.109), kind=kOutput, calls=%fused_computation.5.clone.1 | convolution fusion | flops 542113792 | bytes 606208 | tf_op jit(solution)/shard_map/while/body/eval_jaxpr/csh,csl->chl/dot_general | solution.py:30
  63.8 3.8 %fusion.50 = f32[8,4,128,256]{3,2,1,0:T(8,128)} fusion(f32[8,4,128,256]{3,2,1,0:T(8,128)} %get-tuple-element.116, s32[]{:T(128)S(6)} %copy.30, f32[4,128,256]{2,1,0:T(8,128)S(1)} %fusion.48, s32[4,2048]{1,0:T(4,128)S(1)} %add_select_fusion.5, bf16[4,2048]{1,0:T(4,128)(2,1)S(1)} %fusion.49, s32[4,2048]{1,0:T(4,128)S(1)} %get-tuple-element.109), kind=kOutput, calls=%fused_computation.18.clone.1 | convolution fusion | flops 542244864 | bytes 1130500 | tf_op jit(solution)/shard_map/while/body/eval_jaxpr/csh,csl->chl/dot_general | solution.py:33
  67.7 2.6 %fusion.39 = (f32[128,256]{1,0:T(8,128)S(1)}, f32[128,256]{1,0:T(8,128)S(1)}) fusion(f32[8,4,128,256]{3,2,1,0:T(8,128)} %get-tuple-element.58), kind=kLoop, calls=%fused_computation.62 | loop fusion | flops 3080192 | bytes 4456448 | tf_op jit(solution)/shard_map/reduce_sum | solution.py:61
  70.6 0.9 pad_maximum_fusion
  71.6 4.4 %copy.26 = bf16[4,8,128,256]{3,1,2,0:T(8,128)(2,1)S(1)} copy(f32[4,8,128,256]{3,2,1,0:T(8,128)} %bitcast.62) | data formatting | bytes 6291456
  76.0 6.0 %copy.21 = bf16[32,32768]{0,1:T(8,128)(2,1)} copy(bf16[32,32768]{1,0:T(8,128)(2,1)S(1)} %bitcast.63) | data formatting | bytes 4194304 | tf_op jit(solution)/shard_map/reshape | solution.py:60
  82.0 10.1 %gather_fusion = bf16[2048,32]{1,0:T(8,128)(2,1)S(1)} fusion(bf16[32,32768]{0,1:T(8,128)(2,1)} %copy.21, s32[2048]{0:T(1024)S(1)} %fusion.38), kind=kCustom, calls=%fused_computation | custom fusion | bytes 270336 | tf_op jit(solution)/shard_map/jit(_take)/gather | solution.py:73
  92.3 0.7 select_convert_fusion
  93.0 4.3 %all-to-all-start = ((bf16[32,2,1024]{2,0,1:T(8,128)(2,1)}), bf16[32,2,1024]{2,0,1:T(8,128)(2,1)S(1)}, u32[]{:S(2)}, u32[]{:S(2)}) async-start(bf16[32,2,1024]{2,0,1:T(8,128)(2,1)} %select_convert_fusion), calls=%async_computation | async-start | bytes 262144 | tf_op jit(solution)/shard_map/all_to_all | solution.py:79
  97.3 103.7 %all-reduce.2.cloned.1.call-done = f32[2,32768]{1,0:T(2,128)} async-done(((f32[2,32768]{1,0:T(2,128)}), f32[2,32768]{1,0:T(2,128)}) %all-reduce.2.cloned.1.call-update) | async-done | bytes 262160 | tf_op jit(solution)/shard_map/psum | solution.py:65
  201.0 8.9 %copy.23 = f32[2,32768]{0,1:T(8,128)} copy(f32[2,32768]{1,0:T(2,128)} %all-reduce.2.cloned.1.call-done) | data formatting | bytes 524288 | tf_op jit(solution)/shard_map/psum | solution.py:65
  209.9 11.2 %gather_fusion.1 = f32[2048,2]{1,0:T(8,128)S(1)} fusion(f32[2,32768]{0,1:T(8,128)} %copy.23, s32[2048]{0:T(1024)S(1)} %fusion.38), kind=kCustom, calls=%fused_computation.1 | custom fusion | bytes 40960 | tf_op jit(solution)/shard_map/jit(_take)/gather | solution.py:67
  221.7 0.8 pad_maximum_fusion.1
  223.2 0.7 fusion.34
  (53 shorter events, 2.9 us)
Async XLA Ops:
  7.2 193.8 %all-reduce.2.cloned.1.call-start = ((), (), s32[]{:S(2)}) async-start(), calls=%async_computation.1 | async-start | bytes 524288 | tf_op jit(solution)/shard_map/psum | solution.py:65
  67.7 3.9 %copy-start.1 = (s32[2048]{0:T(1024)S(1)}, s32[2048]{0:T(1024)}, u32[]{:S(2)}) copy-start(s32[2048]{0:T(1024)} %param.9) | copy-start | bytes 24580
  93.0 130.2 %all-to-all-start = ((bf16[32,2,1024]{2,0,1:T(8,128)(2,1)}), bf16[32,2,1024]{2,0,1:T(8,128)(2,1)S(1)}, u32[]{:S(2)}, u32[]{:S(2)}) async-start(bf16[32,2,1024]{2,0,1:T(8,128)(2,1)} %select_convert_fusion), calls=%async_computation | async-start | bytes 262144 | tf_op jit(solution)/shard_map/all_to_all | solution.py:79
  201.0 20.5 %copy-start = (f32[2,32768]{1,0:T(2,128)S(1)}, f32[2,32768]{1,0:T(2,128)}, u32[]{:S(2)}) copy-start(f32[2,32768]{1,0:T(2,128)} %all-reduce.2.cloned.1.call-done) | copy-start | bytes 786436
Sparse Core Ops, SparseCore 0:
  71.7 129.2 all-reduce.1
where the time goes:
time: 231 us
  waiting for transfers between devices  104 us (45%)
  matrix products  55.7 us (24%)
  local copies, waits for them, and re-layouts  41.3 us (18%)
  between operations  14.2 us (6%)
  other arithmetic  11.3 us (5%)
  starting transfers between devices  4.31 us (2%)
    psum x1, waiting for transfers between devices, per_device(): sums = lax.psum(terms, ('gx', 'gy', 'gz'))  104 us
    dot_general x8, matrix products, cell_block(): jnp.einsum('csh,csl->chl', high_table, lower_table, preferred_element_typ...  30.5 us
    dot_general x8, matrix products, cell_block(): jnp.einsum('csh,csl->chl', high_table, upper_table, preferred_element_typ...  25.2 us
    gather x1, local copies, waits for them, and re-layouts, per_device(): picked_sums = jnp.take(sums, selected, axis=1)  11.2 us
    gather x2, local copies, waits for them, and re-layouts, per_device(): dense = jnp.take(expanded, selected, axis=1)  10.3 us
    psum x1, local copies, waits for them, and re-layouts, per_device(): sums = lax.psum(terms, ('gx', 'gy', 'gz'))  8.92 us
    reshape x1, local copies, waits for them, and re-layouts, per_device(): expanded = expanded.reshape(local_cells, GENES)  5.99 us
    unnamed x7, local copies, waits for them, and re-layouts  4.7 us
  transfers between devices with their start and end apart: 2, of which 1 were waited for; matrix products, arithmetic and copies ran while one was open for 19% of the time, Pallas kernels for 0%

commit v1 on v0

--- a/solution.py
+++ b/solution.py
@@ -62,7 +62,7 @@
     square = jnp.sum(expanded * expanded, axis=0)
     terms = jnp.stack([total, square])
     owned = GENES // owners
-    sums = lax.psum(terms, ("gx", "gy", "gz"))
+    sums = lax.all_gather(terms, axis_name=("gx", "gy", "gz")).sum(axis=0)
     own_sums = lax.dynamic_slice_in_dim(sums, owner_index * owned, owned, 1)
     picked_sums = jnp.take(sums, selected, axis=1)
     own_mean = own_sums[0] / cells

time: 231 us -> 187 us (0.81)
  waiting for transfers between devices: 104 us -> 54.2 us
  other arithmetic: 11.3 us -> 17.3 us
    psum x1 -> x0, waiting for transfers between devices: 104 us -> none  [per_device(): sums = lax.psum(terms, ('gx', 'gy', 'gz'))]
    all_gather x0 -> x1, waiting for transfers between devices: none -> 54.2 us  [per_device(): sums = lax.all_gather(terms, axis_name=('gx', 'gy', 'gz')).sum(axis=0)]
    psum x1 -> x0, local copies, waits for them, and re-layouts: 8.92 us -> none  [per_device(): sums = lax.psum(terms, ('gx', 'gy', 'gz'))]
    reduce_sum x0 -> x1, local copies, waits for them, and re-layouts: none -> 8.34 us  [per_device(): sums = lax.all_gather(terms, axis_name=('gx', 'gy', 'gz')).sum(axis=0)]
    reduce_sum x0 -> x1, other arithmetic: none -> 6.1 us  [per_device(): sums = lax.all_gather(terms, axis_name=('gx', 'gy', 'gz')).sum(axis=0)]
    unnamed x7 -> x5, local copies, waits for them, and re-layouts: 4.7 us -> 4.7 us
  transfers between devices with their start and end apart: 2 -> 2, of which waited for: 1 -> 1; matrix products, arithmetic and copies ran while one was open for 19% -> 26% of each run, Pallas kernels for 0% -> 0%
where the time goes in v1:
time: 187 us
  matrix products  55.7 us (30%)
  waiting for transfers between devices  54.2 us (29%)
  local copies, waits for them, and re-layouts  40.9 us (22%)
  other arithmetic  17.3 us (9%)
  between operations  14.1 us (8%)
  starting transfers between devices  4.19 us (2%)
    all_gather x1, waiting for transfers between devices, per_device(): sums = lax.all_gather(terms, axis_name=('gx', 'gy', 'gz')).sum(axis=0)  54.2 us
    dot_general x8, matrix products, cell_block(): jnp.einsum('csh,csl->chl', high_table, lower_table, preferred_element_typ...  30.4 us
    dot_general x8, matrix products, cell_block(): jnp.einsum('csh,csl->chl', high_table, upper_table, preferred_element_typ...  25.2 us
    gather x1, local copies, waits for them, and re-layouts, per_device(): picked_sums = jnp.take(sums, selected, axis=1)  11.2 us
    gather x2, local copies, waits for them, and re-layouts, per_device(): dense = jnp.take(expanded, selected, axis=1)  10.4 us
    reduce_sum x1, local copies, waits for them, and re-layouts, per_device(): sums = lax.all_gather(terms, axis_name=('gx', 'gy', 'gz')).sum(axis=0)  8.34 us
    reduce_sum x1, other arithmetic, per_device(): sums = lax.all_gather(terms, axis_name=('gx', 'gy', 'gz')).sum(axis=0)  6.1 us
    reshape x1, local copies, waits for them, and re-layouts, per_device(): expanded = expanded.reshape(local_cells, GENES)  6.04 us
  transfers between devices with their start and end apart: 2, of which 1 were waited for; matrix products, arithmetic and copies ran while one was open for 26% of the time, Pallas kernels for 0%

profile of v1, /device:TPU:0, one launch (start us, length us, event | category | flops | bytes accessed | tf_op | source)
XLA Modules:
  0.0 186.8 jit_solution(16777828010177647213)
XLA Ops:
  7.2 1.2 fusion.36
  8.4 1.1 multiply_log-plus-one_fusion
  9.6 1.0 fusion.35
  10.8 56.9 %while.12 = (s32[]{:T(128)}, f32[8,4,128,256]{3,2,1,0:T(8,128)}, s32[8,4,2048]{2,1,0:T(4,128)S(1)}, f32[8,4,2048]{2,1,0:T(4,128)S(1)}, s32[]{:T(128)}) while((s32[]{:T(128)}, f32[8,4,128,256]{3,2,1,0:T(8,128)}, s32[8,4,2048]{2,1,0:T(4,128)S(1)}, f32[8,4,2048]{2,1,0:T(4,128)S(1)}, s32[]{:T(128)}) %tuple.39), condition=%wide.region_2.3_spmd, body=%wide.region_1.2_spmd.sunk | while | flops 1084588032 | bytes 1982553 | solution.py:53
  10.9 3.2 %fusion.48 = f32[4,128,256]{2,1,0:T(8,128)S(1)} fusion(s32[4,2048]{1,0:T(4,128)S(1)} %add_select_fusion.5, bf16[4,2048]{1,0:T(4,128)(2,1)S(1)} %bitcast_convert_fusion.2, s32[4,2048]{1,0:T(4,128)S(1)} %get-tuple-element.109), kind=kOutput, calls=%fused_computation.5.clone.1 | convolution fusion | flops 542113792 | bytes 606208 | tf_op jit(solution)/shard_map/while/body/eval_jaxpr/csh,csl->chl/dot_general | solution.py:30
  14.1 3.8 %fusion.50 = f32[8,4,128,256]{3,2,1,0:T(8,128)} fusion(f32[8,4,128,256]{3,2,1,0:T(8,128)} %get-tuple-element.116, s32[]{:T(128)S(6)} %copy.27, f32[4,128,256]{2,1,0:T(8,128)S(1)} %fusion.48, s32[4,2048]{1,0:T(4,128)S(1)} %add_select_fusion.5, bf16[4,2048]{1,0:T(4,128)(2,1)S(1)} %fusion.49, s32[4,2048]{1,0:T(4,128)S(1)} %get-tuple-element.109), kind=kOutput, calls=%fused_computation.18.clone.1 | convolution fusion | flops 542244864 | bytes 1130500 | tf_op jit(solution)/shard_map/while/body/eval_jaxpr/csh,csl->chl/dot_general | solution.py:33
  18.0 3.2 %fusion.48 = f32[4,128,256]{2,1,0:T(8,128)S(1)} fusion(s32[4,2048]{1,0:T(4,128)S(1)} %add_select_fusion.5, bf16[4,2048]{1,0:T(4,128)(2,1)S(1)} %bitcast_convert_fusion.2, s32[4,2048]{1,0:T(4,128)S(1)} %get-tuple-element.109), kind=kOutput, calls=%fused_computation.5.clone.1 | convolution fusion | flops 542113792 | bytes 606208 | tf_op jit(solution)/shard_map/while/body/eval_jaxpr/csh,csl->chl/dot_general | solution.py:30
  21.2 3.8 %fusion.50 = f32[8,4,128,256]{3,2,1,0:T(8,128)} fusion(f32[8,4,128,256]{3,2,1,0:T(8,128)} %get-tuple-element.116, s32[]{:T(128)S(6)} %copy.27, f32[4,128,256]{2,1,0:T(8,128)S(1)} %fusion.48, s32[4,2048]{1,0:T(4,128)S(1)} %add_select_fusion.5, bf16[4,2048]{1,0:T(4,128)(2,1)S(1)} %fusion.49, s32[4,2048]{1,0:T(4,128)S(1)} %get-tuple-element.109), kind=kOutput, calls=%fused_computation.18.clone.1 | convolution fusion | flops 542244864 | bytes 1130500 | tf_op jit(solution)/shard_map/while/body/eval_jaxpr/csh,csl->chl/dot_general | solution.py:33
  25.1 3.2 %fusion.48 = f32[4,128,256]{2,1,0:T(8,128)S(1)} fusion(s32[4,2048]{1,0:T(4,128)S(1)} %add_select_fusion.5, bf16[4,2048]{1,0:T(4,128)(2,1)S(1)} %bitcast_convert_fusion.2, s32[4,2048]{1,0:T(4,128)S(1)} %get-tuple-element.109), kind=kOutput, calls=%fused_computation.5.clone.1 | convolution fusion | flops 542113792 | bytes 606208 | tf_op jit(solution)/shard_map/while/body/eval_jaxpr/csh,csl->chl/dot_general | solution.py:30
  28.3 3.8 %fusion.50 = f32[8,4,128,256]{3,2,1,0:T(8,128)} fusion(f32[8,4,128,256]{3,2,1,0:T(8,128)} %get-tuple-element.116, s32[]{:T(128)S(6)} %copy.27, f32[4,128,256]{2,1,0:T(8,128)S(1)} %fusion.48, s32[4,2048]{1,0:T(4,128)S(1)} %add_select_fusion.5, bf16[4,2048]{1,0:T(4,128)(2,1)S(1)} %fusion.49, s32[4,2048]{1,0:T(4,128)S(1)} %get-tuple-element.109), kind=kOutput, calls=%fused_computation.18.clone.1 | convolution fusion | flops 542244864 | bytes 1130500 | tf_op jit(solution)/shard_map/while/body/eval_jaxpr/csh,csl->chl/dot_general | solution.py:33
  32.2 3.2 %fusion.48 = f32[4,128,256]{2,1,0:T(8,128)S(1)} fusion(s32[4,2048]{1,0:T(4,128)S(1)} %add_select_fusion.5, bf16[4,2048]{1,0:T(4,128)(2,1)S(1)} %bitcast_convert_fusion.2, s32[4,2048]{1,0:T(4,128)S(1)} %get-tuple-element.109), kind=kOutput, calls=%fused_computation.5.clone.1 | convolution fusion | flops 542113792 | bytes 606208 | tf_op jit(solution)/shard_map/while/body/eval_jaxpr/csh,csl->chl/dot_general | solution.py:30
  35.4 3.8 %fusion.50 = f32[8,4,128,256]{3,2,1,0:T(8,128)} fusion(f32[8,4,128,256]{3,2,1,0:T(8,128)} %get-tuple-element.116, s32[]{:T(128)S(6)} %copy.27, f32[4,128,256]{2,1,0:T(8,128)S(1)} %fusion.48, s32[4,2048]{1,0:T(4,128)S(1)} %add_select_fusion.5, bf16[4,2048]{1,0:T(4,128)(2,1)S(1)} %fusion.49, s32[4,2048]{1,0:T(4,128)S(1)} %get-tuple-element.109), kind=kOutput, calls=%fused_computation.18.clone.1 | convolution fusion | flops 542244864 | bytes 1130500 | tf_op jit(solution)/shard_map/while/body/eval_jaxpr/csh,csl->chl/dot_general | solution.py:33
  39.3 3.2 %fusion.48 = f32[4,128,256]{2,1,0:T(8,128)S(1)} fusion(s32[4,2048]{1,0:T(4,128)S(1)} %add_select_fusion.5, bf16[4,2048]{1,0:T(4,128)(2,1)S(1)} %bitcast_convert_fusion.2, s32[4,2048]{1,0:T(4,128)S(1)} %get-tuple-element.109), kind=kOutput, calls=%fused_computation.5.clone.1 | convolution fusion | flops 542113792 | bytes 606208 | tf_op jit(solution)/shard_map/while/body/eval_jaxpr/csh,csl->chl/dot_general | solution.py:30
  42.5 3.8 %fusion.50 = f32[8,4,128,256]{3,2,1,0:T(8,128)} fusion(f32[8,4,128,256]{3,2,1,0:T(8,128)} %get-tuple-element.116, s32[]{:T(128)S(6)} %copy.27, f32[4,128,256]{2,1,0:T(8,128)S(1)} %fusion.48, s32[4,2048]{1,0:T(4,128)S(1)} %add_select_fusion.5, bf16[4,2048]{1,0:T(4,128)(2,1)S(1)} %fusion.49, s32[4,2048]{1,0:T(4,128)S(1)} %get-tuple-element.109), kind=kOutput, calls=%fused_computation.18.clone.1 | convolution fusion | flops 542244864 | bytes 1130500 | tf_op jit(solution)/shard_map/while/body/eval_jaxpr/csh,csl->chl/dot_general | solution.py:33
  46.5 3.2 %fusion.48 = f32[4,128,256]{2,1,0:T(8,128)S(1)} fusion(s32[4,2048]{1,0:T(4,128)S(1)} %add_select_fusion.5, bf16[4,2048]{1,0:T(4,128)(2,1)S(1)} %bitcast_convert_fusion.2, s32[4,2048]{1,0:T(4,128)S(1)} %get-tuple-element.109), kind=kOutput, calls=%fused_computation.5.clone.1 | convolution fusion | flops 542113792 | bytes 606208 | tf_op jit(solution)/shard_map/while/body/eval_jaxpr/csh,csl->chl/dot_general | solution.py:30
  49.6 3.8 %fusion.50 = f32[8,4,128,256]{3,2,1,0:T(8,128)} fusion(f32[8,4,128,256]{3,2,1,0:T(8,128)} %get-tuple-element.116, s32[]{:T(128)S(6)} %copy.27, f32[4,128,256]{2,1,0:T(8,128)S(1)} %fusion.48, s32[4,2048]{1,0:T(4,128)S(1)} %add_select_fusion.5, bf16[4,2048]{1,0:T(4,128)(2,1)S(1)} %fusion.49, s32[4,2048]{1,0:T(4,128)S(1)} %get-tuple-element.109), kind=kOutput, calls=%fused_computation.18.clone.1 | convolution fusion | flops 542244864 | bytes 1130500 | tf_op jit(solution)/shard_map/while/body/eval_jaxpr/csh,csl->chl/dot_general | solution.py:33
  53.5 3.2 %fusion.48 = f32[4,128,256]{2,1,0:T(8,128)S(1)} fusion(s32[4,2048]{1,0:T(4,128)S(1)} %add_select_fusion.5, bf16[4,2048]{1,0:T(4,128)(2,1)S(1)} %bitcast_convert_fusion.2, s32[4,2048]{1,0:T(4,128)S(1)} %get-tuple-element.109), kind=kOutput, calls=%fused_computation.5.clone.1 | convolution fusion | flops 542113792 | bytes 606208 | tf_op jit(solution)/shard_map/while/body/eval_jaxpr/csh,csl->chl/dot_general | solution.py:30
  56.7 3.8 %fusion.50 = f32[8,4,128,256]{3,2,1,0:T(8,128)} fusion(f32[8,4,128,256]{3,2,1,0:T(8,128)} %get-tuple-element.116, s32[]{:T(128)S(6)} %copy.27, f32[4,128,256]{2,1,0:T(8,128)S(1)} %fusion.48, s32[4,2048]{1,0:T(4,128)S(1)} %add_select_fusion.5, bf16[4,2048]{1,0:T(4,128)(2,1)S(1)} %fusion.49, s32[4,2048]{1,0:T(4,128)S(1)} %get-tuple-element.109), kind=kOutput, calls=%fused_computation.18.clone.1 | convolution fusion | flops 542244864 | bytes 1130500 | tf_op jit(solution)/shard_map/while/body/eval_jaxpr/csh,csl->chl/dot_general | solution.py:33
  60.7 3.2 %fusion.48 = f32[4,128,256]{2,1,0:T(8,128)S(1)} fusion(s32[4,2048]{1,0:T(4,128)S(1)} %add_select_fusion.5, bf16[4,2048]{1,0:T(4,128)(2,1)S(1)} %bitcast_convert_fusion.2, s32[4,2048]{1,0:T(4,128)S(1)} %get-tuple-element.109), kind=kOutput, calls=%fused_computation.5.clone.1 | convolution fusion | flops 542113792 | bytes 606208 | tf_op jit(solution)/shard_map/while/body/eval_jaxpr/csh,csl->chl/dot_general | solution.py:30
  63.8 3.8 %fusion.50 = f32[8,4,128,256]{3,2,1,0:T(8,128)} fusion(f32[8,4,128,256]{3,2,1,0:T(8,128)} %get-tuple-element.116, s32[]{:T(128)S(6)} %copy.27, f32[4,128,256]{2,1,0:T(8,128)S(1)} %fusion.48, s32[4,2048]{1,0:T(4,128)S(1)} %add_select_fusion.5, bf16[4,2048]{1,0:T(4,128)(2,1)S(1)} %fusion.49, s32[4,2048]{1,0:T(4,128)S(1)} %get-tuple-element.109), kind=kOutput, calls=%fused_computation.18.clone.1 | convolution fusion | flops 542244864 | bytes 1130500 | tf_op jit(solution)/shard_map/while/body/eval_jaxpr/csh,csl->chl/dot_general | solution.py:33
  67.6 2.6 %fusion.39 = (f32[128,256]{1,0:T(8,128)S(1)}, f32[128,256]{1,0:T(8,128)S(1)}) fusion(f32[8,4,128,256]{3,2,1,0:T(8,128)} %get-tuple-element.58), kind=kLoop, calls=%fused_computation.62 | loop fusion | flops 3080192 | bytes 4456448 | tf_op jit(solution)/shard_map/reduce_sum | solution.py:61
  70.6 0.9 maximum_bitcast_fusion
  71.6 4.4 %copy.23 = bf16[4,8,128,256]{3,1,2,0:T(8,128)(2,1)S(1)} copy(f32[4,8,128,256]{3,2,1,0:T(8,128)} %bitcast.64) | data formatting | bytes 6291456
  76.0 6.0 %copy.18 = bf16[32,32768]{0,1:T(8,128)(2,1)} copy(bf16[32,32768]{1,0:T(8,128)(2,1)S(1)} %bitcast.65) | data formatting | bytes 4194304 | tf_op jit(solution)/shard_map/reshape | solution.py:60
  82.0 10.2 %gather_fusion = bf16[2048,32]{1,0:T(8,128)(2,1)S(1)} fusion(bf16[32,32768]{0,1:T(8,128)(2,1)} %copy.18, s32[2048]{0:T(1024)S(1)} %fusion.38), kind=kCustom, calls=%fused_computation | custom fusion | bytes 270336 | tf_op jit(solution)/shard_map/jit(_take)/gather | solution.py:73
  93.2 4.2 %all-to-all-start = ((bf16[32,2,1024]{2,0,1:T(8,128)(2,1)}), bf16[32,2,1024]{2,0,1:T(8,128)(2,1)S(1)}, u32[]{:S(2)}, u32[]{:S(2)}) async-start(bf16[32,2,1024]{2,0,1:T(8,128)(2,1)} %select_convert_fusion), calls=%async_computation | async-start | bytes 262144 | tf_op jit(solution)/shard_map/all_to_all | solution.py:79
  97.3 54.2 %all-gather.4.cloned.1.call-done = f32[32,2,32768]{2,1,0:T(2,128)} async-done(((f32[1,2,32768]{2,1,0:T(2,128)}), f32[32,2,32768]{2,1,0:T(2,128)}) %all-gather.4.cloned.1.call-update) | async-done | bytes 8388624 | tf_op jit(solution)/shard_map/all_gather | solution.py:65
  151.5 6.1 %reduce_sum.39 = f32[2,32768]{1,0:T(2,128)S(1)} reduce(f32[32,2,32768]{2,1,0:T(2,128)} %all-gather.4.cloned.1.call-done, f32[]{:T(128)} %constant.110.clone.1), dimensions={0}, to_apply=%region_5.6 | reduce | flops 2031616 | bytes 8650756 | tf_op jit(solution)/shard_map/reduce_sum | solution.py:65
  157.6 8.3 %copy.20 = f32[2,32768]{0,1:T(8,128)} copy(f32[2,32768]{1,0:T(2,128)S(1)} %reduce_sum.39) | data formatting | bytes 524288 | tf_op jit(solution)/shard_map/reduce_sum | solution.py:65
  165.9 11.2 %gather_fusion.1 = f32[2048,2]{1,0:T(8,128)S(1)} fusion(f32[2,32768]{0,1:T(8,128)} %copy.20, s32[2048]{0:T(1024)S(1)} %fusion.38), kind=kCustom, calls=%fused_computation.1 | custom fusion | bytes 40960 | tf_op jit(solution)/shard_map/jit(_take)/gather | solution.py:67
  177.7 0.8 pad_maximum_fusion
  179.2 0.7 fusion.34
  (52 shorter events, 3.6 us)
Async XLA Ops:
  7.2 144.3 %all-gather.4.cloned.1.call-start = ((), (), s32[]{:S(2)}) async-start(), calls=%async_computation.1 | async-start | bytes 8650752 | tf_op jit(solution)/shard_map/all_gather | solution.py:65
  67.6 3.9 %copy-start = (s32[2048]{0:T(1024)S(1)}, s32[2048]{0:T(1024)}, u32[]{:S(2)}) copy-start(s32[2048]{0:T(1024)} %param.9) | copy-start | bytes 24580
  93.2 86.1 %all-to-all-start = ((bf16[32,2,1024]{2,0,1:T(8,128)(2,1)}), bf16[32,2,1024]{2,0,1:T(8,128)(2,1)S(1)}, u32[]{:S(2)}, u32[]{:S(2)}) async-start(bf16[32,2,1024]{2,0,1:T(8,128)(2,1)} %select_convert_fusion), calls=%async_computation | async-start | bytes 262144 | tf_op jit(solution)/shard_map/all_to_all | solution.py:79
Sparse Core Ops, SparseCore 0:
  71.7 79.7 all-gather.3
